TPU v7x, 32 devices: a whole 2x2x4 slice. The times are simulated.
32 devices in a mesh: ctx: 32 (over z, y, x, core).
Axes of the slice: x: 2, y: 2, z: 4, core: 2. Of those that a mesh axis runs over, the one named last changes fastest.
Arguments:
- queries: bfloat16 [8192, 768], P('ctx'), may hold values from -16 to 16
- keys: bfloat16 [8192, 768], P('ctx'), may hold values from -16 to 16
- values: bfloat16 [8192, 768], P('ctx'), may hold values from -6 to 6
- offsets: int32 [5, 12], replicated, may hold values from 0 to 31, as said below
Outputs:
- attended: bfloat16 [8192, 768], P('ctx')
Inputs may be any that keep to these rules, and one draw needn't show every extreme that they name: offsets[l, h] lies in 0 to min(4 ** l, 32) - 1.
All inputs are finite; a program needn't handle non-finite values.
Results may differ from a plain program's by a relative error of at most 0.0035.
Values may be sent and summed in bfloat16 or wider, within the bound.
A program may use at most 64 MiB of HBM per device.

v0:
```python
import jax
import jax.numpy as jnp
from jax import lax
from jax.sharding import PartitionSpec as P


def swapped(value, axis, distance):
    mask = 2**distance
    pairs = [(source, source ^ mask) for source in range(lax.axis_size(axis))]
    return lax.ppermute(value, axis, pairs)


def attend_rows(query_rows, key_rows, value_rows, query_pos, key_pos, heads, scale):
    rows = query_rows.shape[0]
    cols = key_rows.shape[0]
    head_size = query_rows.shape[1] // heads
    query_heads = query_rows.reshape(rows, heads, head_size)
    key_heads = key_rows.reshape(cols, heads, head_size)
    value_heads = value_rows.reshape(cols, heads, head_size)
    allowed = key_pos[None, :] <= query_pos[:, None]
    scores = (
        jnp.einsum("qhd,khd->hqk", query_heads, key_heads, preferred_element_type=jnp.float32)
        * scale
    )
    scores = jnp.where(allowed[None], scores, -1e30)
    peak = jnp.max(scores, axis=2)
    weights = jnp.where(allowed[None], jnp.exp(scores - peak[:, :, None]), 0.0)
    totals = jnp.sum(weights, axis=2)
    result = jnp.einsum(
        "hqk,khd->qhd",
        weights.astype(jnp.bfloat16),
        value_heads,
        preferred_element_type=jnp.float32,
    )
    return (result / totals.T[:, :, None], (peak + jnp.log(totals)).T)


def causal_blocks(query_rows, key_rows, value_rows, heads, scale):
    length = query_rows.shape[0]
    block = min(512, length)
    query_pos = jnp.arange(0, block, dtype=jnp.int32)
    key_pos = jnp.arange(block, dtype=jnp.int32)
    result, lse_part = attend_rows(
        query_rows, key_rows, value_rows, query_pos, key_pos, heads, scale
    )
    return (result, lse_part)


def select_rows(source, offset_row, group, heads):
    count = source.shape[0]
    head_size = source.shape[1] // heads
    shaped = source.reshape(count // group, group, heads, head_size)
    hit = jnp.arange(group, dtype=jnp.int32)[:, None] == offset_row[None, :]
    picked = jnp.sum(jnp.where(hit[None, :, :, None], shaped, jnp.zeros((), source.dtype)), axis=1)
    return picked.reshape(count // group, heads * head_size)


def merge_levels(base_out, base_lse, extras):
    rows_all, heads, head_size = base_out.shape
    best = base_lse
    numer = base_out
    denom = jnp.ones(base_lse.shape, jnp.float32)
    for level_out, level_lse, offset_row, group in extras:
        rows = level_out.shape[0]
        hit = jnp.arange(group, dtype=jnp.int32)[:, None] == offset_row[None, :]
        best_g = best.reshape(rows, group, heads)
        lse_g = jnp.where(hit[None], level_lse[:, None], -1e30)
        newest = jnp.maximum(best_g, lse_g)
        keep_old = jnp.exp(best_g - newest)
        take_new = jnp.exp(lse_g - newest)
        numer = (
            numer.reshape(rows, group, heads, head_size) * keep_old[..., None]
            + level_out[:, None] * take_new[..., None]
        ).reshape(rows_all, heads, head_size)
        denom = (denom.reshape(rows, group, heads) * keep_old + take_new).reshape(rows_all, heads)
        best = newest.reshape(rows_all, heads)
    merged = numer / denom[..., None]
    return merged.reshape(rows_all, -1).astype(jnp.bfloat16)


def place_pair(mine, arrived, position, bit_pos):
    upper = jnp.right_shift(position, bit_pos) % 2 == 1
    first = jnp.where(upper, arrived, mine)
    second = jnp.where(upper, mine, arrived)
    return jnp.concatenate([first, second], 1)


def double_rows(stacked, group, position):
    for bit_pos in range(group.bit_length() - 1):
        arrived = swapped(stacked, "ctx", bit_pos)
        stacked = place_pair(stacked, arrived, position, bit_pos)
    return stacked


def body(queries, keys, values, offsets):
    tokens, width = queries.shape
    heads = offsets.shape[1]
    levels = offsets.shape[0]
    scale = (width // heads) ** (-0.5)
    count = lax.axis_size("ctx")
    position = lax.axis_index("ctx")
    base_out, base_lse = causal_blocks(queries, keys, values, heads, scale)
    groups = [min(4**height, count) for height in range(levels)]
    query_sel = [None]
    stacks = [None]
    for height in range(1, levels):
        query_sel.append(select_rows(queries, offsets[height], groups[height], heads))
        stacks.append(
            jnp.stack(
                [
                    select_rows(keys, offsets[height], groups[height], heads),
                    select_rows(values, offsets[height], groups[height], heads),
                ]
            )
        )
    direct = list(range(1, levels))
    for height in direct:
        stacks[height] = double_rows(stacks[height], groups[height], position)
    extras = []
    for height in range(1, levels):
        group = groups[height]
        rows = tokens // group
        query_pos = position % group * rows + jnp.arange(rows, dtype=jnp.int32)
        key_pos = jnp.arange(tokens, dtype=jnp.int32)
        level_out, level_lse = attend_rows(
            query_sel[height],
            stacks[height][0],
            stacks[height][1],
            query_pos,
            key_pos,
            heads,
            scale,
        )
        extras.append((level_out, level_lse, offsets[height], group))
    return merge_levels(base_out, base_lse, extras)


def solution(mesh):
    in_specs = (P("ctx", None), P("ctx", None), P("ctx", None), P())
    out_specs = P("ctx", None)
    return jax.shard_map(body, mesh=mesh, in_specs=in_specs, out_specs=out_specs, check_vma=False)
```

profile of v0, /device:TPU:0, one launch (start us, length us, event | category | flops | bytes accessed | tf_op | source)
XLA Modules:
  0.0 156.8 jit_solution(3004068343948117945)
XLA Ops:
  2.5 1.7 %reshape.600 = bf16[16,16,12,64]{3,2,1,0:T(8,128)(2,1)S(1)} reshape(bf16[256,768]{1,0:T(8,128)(2,1)} %param.5) | data formatting | bytes 786432 | tf_op jit(solution)/shard_map/reshape | solution.py:52
  5.9 2.9 %select_reduce_fusion.8 = (bf16[16,12,64]{2,1,0:T(8,128)(2,1)}, bf16[16,12,64]{2,1,0:T(8,128)(2,1)S(1)}, bf16[16,12,64]{2,1,0:T(8,128)(2,1)S(1)}) fusion(bf16[16,16,12,64]{3,2,1,0:T(8,128)(2,1)S(1)} %reshape.599, pred[16,12]{1,0:T(8,128)(4,1)S(1)} %iota_compare_fusion.6, bf16[16,16,12,64]{3,2,1,0:T(8,128)(2,1)S(1)} %reshape.600, ...), kind=kLoop, calls=%fused_computation.32 | loop fusion | flops 1142784 | bytes 1253568 | tf_op jit(solution)/shard_map/reduce_sum | solution.py:54
  13.5 3.5 %select_reduce_fusion.11 = (bf16[64,12,64]{2,1,0:T(8,128)(2,1)}, bf16[64,12,64]{2,1,0:T(8,128)(2,1)}, bf16[64,12,64]{2,1,0:T(8,128)(2,1)S(1)}) fusion(bf16[64,4,12,64]{3,2,1,0:T(8,128)(2,1)S(1)} %reshape.596, pred[4,12]{1,0:T(4,128)(4,1)S(1)} %iota_compare_fusion.7, bf16[64,4,12,64]{3,2,1,0:T(8,128)(2,1)S(1)} %reshape.597, bf16[64,4,12,64]{3,2,1,0:T(8,128)(2,1)} %reshape.598), kind=kLoop, calls=%fused_computation.35 | loop fusion | flops 1032192 | bytes 1474608 | tf_op jit(solution)/shard_map/reduce_sum | solution.py:54
  22.4 3.9 %select_reduce_fusion.4 = (bf16[8,12,64]{2,1,0:T(8,128)(2,1)S(1)}, bf16[8,12,64]{2,1,0:T(8,128)(2,1)S(1)}, bf16[8,12,64]{2,1,0:T(8,128)(2,1)}, bf16[8,12,64]{2,1...) fusion(bf16[8,32,12,64]{3,2,1,0:T(8,128)(2,1)S(1)} %reshape.603, ...), kind=kLoop, calls=%fused_computation.28 | loop fusion | flops 2322432 | bytes 1254144 | tf_op jit(solution)/shard_map/reduce_sum | solution.py:54
  33.5 1.8 %fusion = (f32[12,256]{1,0:T(8,128)S(1)}, f32[12,256,256]{1,2,0:T(8,128)S(1)}) fusion(pred[256,256]{0,1:T(8,128)(4,1)} %iota_compare_fusion, bf16[256,12,64]{0,2,1:T(8,128)(2,1)} %bitcast.119, bf16[256,12,64]{0,2,1:T(8,128)(2,1)} %bitcast.120), kind=kOutput, calls=%fused_computation.2 | convolution fusion | flops 103019520 | bytes 4009984 | tf_op jit(solution)/shard_map/qhd,khd->hqk/dot_general | solution.py:22
  43.0 3.0 %collective-permute-start.7 = (bf16[2,16,768]{2,1,0:T(8,128)(2,1)S(1)}, bf16[2,16,768]{2,1,0:T(8,128)(2,1)S(1)}, u32[]{:S(2)}, u32[]{:S(2)}) collective-permute-start(bf16[2,16,768]{2,1,0:T(8,128)(2,1)S(1)} %pad_maximum_fusion.14), channel_id=1, source_target_pairs={{0,2},{1,3},{2,0},{3,1},{4,6},{5,7},{6,4},{7,5},{8,10},{9,11},{10,... | collective-permute-start | bytes 147464 | tf_op jit(solution)/shard_map/ppermute | solution.py:10
  47.8 2.1 %collective-permute-start.3 = (bf16[2,32,768]{2,1,0:T(8,128)(2,1)S(1)}, bf16[2,32,768]{2,1,0:T(8,128)(2,1)S(1)}, u32[]{:S(2)}, u32[]{:S(2)}) collective-permute-start(bf16[2,32,768]{2,1,0:T(8,128)(2,1)S(1)} %pad_maximum_fusion.11), channel_id=1, source_target_pairs={{0,2},{1,3},{2,0},{3,1},{4,6},{5,7},{6,4},{7,5},{8,10},{9,11},{10,... | collective-permute-start | bytes 294920 | tf_op jit(solution)/shard_map/ppermute | solution.py:10
  63.9 2.6 %collective-permute-start.10 = (bf16[2,128,768]{2,1,0:T(8,128)(2,1)}, bf16[2,128,768]{2,1,0:T(8,128)(2,1)}, u32[]{:S(2)}, u32[]{:S(2)}) collective-permute-start(bf16[2,128,768]{2,1,0:T(8,128)(2,1)} %pad_maximum_fusion.6), channel_id=1, source_target_pairs={{0,16},{1,17},{2,18},{3,19},{4,20},{5,21},{6,22},{7,23},{8,24},{9,... | collective-permute-start | bytes 1179656 | tf_op jit(solution)/shard_map/ppermute | solution.py:10
  66.5 7.5 %collective-permute-done.14 = bf16[2,64,768]{2,1,0:T(8,128)(2,1)S(1)} collective-permute-done((bf16[2,64,768]{2,1,0:T(8,128)(2,1)S(1)}, bf16[2,64,768]{2,1,0:T(8,128)(2,1)S(1)}, u32[]{:S(2)}, u32[]{:S(2)}) %collective-permute-start.14) | collective-permute-done | bytes 196640 | tf_op jit(solution)/shard_map/ppermute | solution.py:10
  77.0 1.9 %copy.74 = bf16[1,256,768]{1,2,0:T(8,128)(2,1)} copy(bf16[1,256,768]{2,1,0:T(8,128)(2,1)} %get-tuple-element.34) | data formatting | bytes 786432 | tf_op jit(solution)/shard_map/slice | solution.py:127
  87.9 1.9 %copy.78 = bf16[1,256,768]{1,2,0:T(8,128)(2,1)} copy(bf16[1,256,768]{2,1,0:T(8,128)(2,1)} %get-tuple-element.35) | data formatting | bytes 786432 | tf_op jit(solution)/shard_map/slice | solution.py:128
  89.9 2.3 %fusion.10 = f32[64,12,64]{0,2,1:T(8,128)} fusion(bf16[256,12,64]{0,2,1:T(8,128)(2,1)} %bitcast.124, f32[12,64,256]{2,1,0:T(8,128)} %copy-done.3, f32[12,64]{1,0:T(8,128)} %copy-done.17, pred[64,256]{1,0:T(8,128)(4,1)} %iota_compare_fusion.1, f32[64,12]{0,1:T(8,128)} %bitcast.129), kind=kOutput, calls=%fused_computation.11 | convolution fusion | flops 25804800 | bytes 1398784 | tf_op jit(solution)/shard_map/hqk,khd->qhd/dot_general | solution.py:29
  92.2 1.9 %copy.79 = f32[64,12,64]{2,0,1:T(8,128)} copy(f32[64,12,64]{0,2,1:T(8,128)} %fusion.10) | data formatting | bytes 393216 | tf_op jit(solution)/shard_map/div | solution.py:35
  94.1 2.4 %mul.163 = f32[64,4,12,64]{3,1,0,2:T(4,128)} broadcast(f32[64,12,64]{2,0,1:T(8,128)} %copy.79), dimensions={0,2,3} | broadcast | bytes 983040 | tf_op jit(solution)/shard_map/mul | solution.py:73
  96.6 2.7 %copy.81 = f32[256,12,64]{0,2,1:T(8,128)} copy(f32[256,12,64]{2,0,1:T(8,128)} %bitcast.114) | data formatting | bytes 1572864 | tf_op jit(solution)/shard_map/mul | solution.py:73
  101.5 1.9 %copy.83 = bf16[1,256,768]{1,2,0:T(8,128)(2,1)} copy(bf16[1,256,768]{2,1,0:T(8,128)(2,1)} %get-tuple-element.38) | data formatting | bytes 786432 | tf_op jit(solution)/shard_map/slice | solution.py:127
  109.8 1.9 %copy.85 = bf16[1,256,768]{1,2,0:T(8,128)(2,1)} copy(bf16[1,256,768]{2,1,0:T(8,128)(2,1)} %get-tuple-element.39) | data formatting | bytes 786432 | tf_op jit(solution)/shard_map/slice | solution.py:128
  115.8 2.8 %copy.86 = f32[256,12,64]{0,2,1:T(8,128)} copy(f32[256,12,64]{2,0,1:T(8,128)} %bitcast.111) | data formatting | bytes 1572864 | tf_op jit(solution)/shard_map/mul | solution.py:73
  120.8 1.9 %copy.88 = bf16[1,256,768]{1,2,0:T(8,128)(2,1)} copy(bf16[1,256,768]{2,1,0:T(8,128)(2,1)} %get-tuple-element.43) | data formatting | bytes 786432 | tf_op jit(solution)/shard_map/slice | solution.py:127
  137.3 1.9 %copy.90 = bf16[1,256,768]{1,2,0:T(8,128)(2,1)} copy(bf16[1,256,768]{2,1,0:T(8,128)(2,1)} %get-tuple-element.42) | data formatting | bytes 786432 | tf_op jit(solution)/shard_map/slice | solution.py:128
  141.8 2.8 %copy.91 = f32[256,12,64]{0,2,1:T(8,128)} copy(f32[256,12,64]{2,0,1:T(8,128)} %bitcast.112) | data formatting | bytes 1572864 | tf_op jit(solution)/shard_map/mul | solution.py:73
  148.2 2.7 %copy.96 = f32[256,12,64]{0,2,1:T(8,128)} copy(f32[256,12,64]{2,0,1:T(8,128)} %bitcast.113) | data formatting | bytes 1572864 | tf_op jit(solution)/shard_map/mul | solution.py:73
  151.1 3.8 %fusion.47 = bf16[256,12,64]{0,2,1:T(8,128)(2,1)} fusion(bf16[256,12,64]{0,2,1:T(8,128)(2,1)} %bitcast.122, f32[12,256,256]{1,2,0:T(8,128)S(1)} %get-tuple-element.79, f32[12,256]{1,0:T(8,128)S(1)} %get-tuple-element.78, pred[256,256]{0,1:T(8,128)(4,1)S(1)} %copy-done.11, f32[256,12,64]{0,2,1:T(8,128)} %copy.96, f32[256,12,64]{0,2,1:T(8,128)} %copy.91, ...), kind=kOutput, calls=%fused_computation.46 | convolution fusion | flops 107544576 | bytes 7278592 | tf_op jit(solution)/shard_map/hqk,khd->qhd/dot_general | solution.py:29
  154.9 1.9 %copy.97 = bf16[256,768]{1,0:T(8,128)(2,1)} copy(bf16[256,768]{0,1:T(8,128)(2,1)} %bitcast.123) | data formatting | bytes 786432 | tf_op jit(solution)/shard_map/convert_element_type | solution.py:78
  (196 shorter events, 92.3 us)
Async XLA Ops:
  0.8 7.9 %copy-start.30 = (pred[16,12]{1,0:T(8,128)(4,1)}, pred[16,12]{1,0:T(8,128)(4,1)S(1)}, u32[]{:S(2)}) copy-start(pred[16,12]{1,0:T(8,128)(4,1)S(1)} %iota_compare_fusion.6) | copy-start | bytes 580
  2.5 8.2 %copy-start = (bf16[256,768]{1,0:T(8,128)(2,1)S(1)}, bf16[256,768]{1,0:T(8,128)(2,1)}, u32[]{:S(2)}) copy-start(bf16[256,768]{1,0:T(8,128)(2,1)} %param.4) | copy-start | bytes 1179652
  4.3 7.0 %copy-start.1 = (bf16[256,768]{1,0:T(8,128)(2,1)S(1)}, bf16[256,768]{1,0:T(8,128)(2,1)}, u32[]{:S(2)}) copy-start(bf16[256,768]{1,0:T(8,128)(2,1)} %param.5) | copy-start | bytes 1179652
  10.2 36.7 %collective-permute-start.2 = (bf16[2,16,768]{2,1,0:T(8,128)(2,1)}, bf16[2,16,768]{2,1,0:T(8,128)(2,1)}, u32[]{:S(2)}, u32[]{:S(2)}) collective-permute-start(bf16[2,16,768]{2,1,0:T(8,128)(2,1)} %constant_dynamic-update-slice_fusion.2), channel_id=1, source_target_pairs={{0,1},{1,0},{2,3},{3,2},{4,5},{5,4},{6,7},{7,6},{8,9},{9,8},{10,11... | collective-permute-start | bytes 147464 | tf_op jit(solution)/shard_map/ppermute | solution.py:10
  19.5 39.7 %collective-permute-start = (bf16[2,64,768]{2,1,0:T(8,128)(2,1)}, bf16[2,64,768]{2,1,0:T(8,128)(2,1)}, u32[]{:S(2)}, u32[]{:S(2)}) collective-permute-start(bf16[2,64,768]{2,1,0:T(8,128)(2,1)} %constant_dynamic-update-slice_fusion), channel_id=1, source_target_pairs={{0,1},{1,0},{2,3},{3,2},{4,5},{5,4},{6,7},{7,6},{8,9},{9,8},{10,11... | collective-permute-start | bytes 589832 | tf_op jit(solution)/shard_map/ppermute | solution.py:10
  27.7 14.5 %collective-permute-start.6 = (bf16[2,8,768]{2,1,0:T(8,128)(2,1)}, bf16[2,8,768]{2,1,0:T(8,128)(2,1)}, u32[]{:S(2)}, u32[]{:S(2)}) collective-permute-start(bf16[2,8,768]{2,1,0:T(8,128)(2,1)} %constant_dynamic-update-slice_fusion.4), channel_id=1, source_target_pairs={{0,1},{1,0},{2,3},{3,2},{4,5},{5,4},{6,7},{7,6},{8,9},{9,8},{10,11... | collective-permute-start | bytes 73736 | tf_op jit(solution)/shard_map/ppermute | solution.py:10
  29.6 16.4 %collective-permute-start.11 = (bf16[2,8,768]{2,1,0:T(8,128)(2,1)}, bf16[2,8,768]{2,1,0:T(8,128)(2,1)}, u32[]{:S(2)}, u32[]{:S(2)}) collective-permute-start(bf16[2,8,768]{2,1,0:T(8,128)(2,1)} %constant_dynamic-update-slice_fusion.6), channel_id=1, source_target_pairs={{0,1},{1,0},{2,3},{3,2},{4,5},{5,4},{6,7},{7,6},{8,9},{9,8},{10,11... | collective-permute-start | bytes 73736 | tf_op jit(solution)/shard_map/ppermute | solution.py:10
  43.0 6.8 %collective-permute-start.7 = (bf16[2,16,768]{2,1,0:T(8,128)(2,1)S(1)}, bf16[2,16,768]{2,1,0:T(8,128)(2,1)S(1)}, u32[]{:S(2)}, u32[]{:S(2)}) collective-permute-start(bf16[2,16,768]{2,1,0:T(8,128)(2,1)S(1)} %pad_maximum_fusion.14), channel_id=1, source_target_pairs={{0,2},{1,3},{2,0},{3,1},{4,6},{5,7},{6,4},{7,5},{8,10},{9,11},{10,... | collective-permute-start | bytes 147464 | tf_op jit(solution)/shard_map/ppermute | solution.py:10
  46.8 4.7 %collective-permute-start.12 = (bf16[2,16,768]{2,1,0:T(8,128)(2,1)S(1)}, bf16[2,16,768]{2,1,0:T(8,128)(2,1)S(1)}, u32[]{:S(2)}, u32[]{:S(2)}) collective-permute-start(bf16[2,16,768]{2,1,0:T(8,128)(2,1)S(1)} %pad_maximum_fusion.15), channel_id=1, source_target_pairs={{0,2},{1,3},{2,0},{3,1},{4,6},{5,7},{6,4},{7,5},{8,10},{9,11},{10,... | collective-permute-start | bytes 147464 | tf_op jit(solution)/shard_map/ppermute | solution.py:10
  47.8 5.4 %collective-permute-start.3 = (bf16[2,32,768]{2,1,0:T(8,128)(2,1)S(1)}, bf16[2,32,768]{2,1,0:T(8,128)(2,1)S(1)}, u32[]{:S(2)}, u32[]{:S(2)}) collective-permute-start(bf16[2,32,768]{2,1,0:T(8,128)(2,1)S(1)} %pad_maximum_fusion.11), channel_id=1, source_target_pairs={{0,2},{1,3},{2,0},{3,1},{4,6},{5,7},{6,4},{7,5},{8,10},{9,11},{10,... | collective-permute-start | bytes 294920 | tf_op jit(solution)/shard_map/ppermute | solution.py:10
  49.9 5.6 %collective-permute-start.8 = (bf16[2,32,768]{2,1,0:T(8,128)(2,1)S(1)}, bf16[2,32,768]{2,1,0:T(8,128)(2,1)S(1)}, u32[]{:S(2)}, u32[]{:S(2)}) collective-permute-start(bf16[2,32,768]{2,1,0:T(8,128)(2,1)S(1)} %pad_maximum_fusion.12), channel_id=1, source_target_pairs={{0,4},{1,5},{2,6},{3,7},{4,0},{5,1},{6,2},{7,3},{8,12},{9,13},{10,... | collective-permute-start | bytes 294920 | tf_op jit(solution)/shard_map/ppermute | solution.py:10
  51.5 6.1 %collective-permute-start.13 = (bf16[2,32,768]{2,1,0:T(8,128)(2,1)S(1)}, bf16[2,32,768]{2,1,0:T(8,128)(2,1)S(1)}, u32[]{:S(2)}, u32[]{:S(2)}) collective-permute-start(bf16[2,32,768]{2,1,0:T(8,128)(2,1)S(1)} %pad_maximum_fusion.13), channel_id=1, source_target_pairs={{0,4},{1,5},{2,6},{3,7},{4,0},{5,1},{6,2},{7,3},{8,12},{9,13},{10,... | collective-permute-start | bytes 294920 | tf_op jit(solution)/shard_map/ppermute | solution.py:10
  53.2 7.7 %collective-permute-start.4 = (bf16[2,64,768]{2,1,0:T(8,128)(2,1)S(1)}, bf16[2,64,768]{2,1,0:T(8,128)(2,1)S(1)}, u32[]{:S(2)}, u32[]{:S(2)}) collective-permute-start(bf16[2,64,768]{2,1,0:T(8,128)(2,1)S(1)} %pad_maximum_fusion.8), channel_id=1, source_target_pairs={{0,4},{1,5},{2,6},{3,7},{4,0},{5,1},{6,2},{7,3},{8,12},{9,13},{10,... | collective-permute-start | bytes 589832 | tf_op jit(solution)/shard_map/ppermute | solution.py:10
  55.6 7.4 %collective-permute-start.9 = (bf16[2,64,768]{2,1,0:T(8,128)(2,1)S(1)}, bf16[2,64,768]{2,1,0:T(8,128)(2,1)S(1)}, u32[]{:S(2)}, u32[]{:S(2)}) collective-permute-start(bf16[2,64,768]{2,1,0:T(8,128)(2,1)S(1)} %pad_maximum_fusion.9), channel_id=1, source_target_pairs={{0,8},{1,9},{2,10},{3,11},{4,12},{5,13},{6,14},{7,15},{8,0},{9,1},... | collective-permute-start | bytes 589832 | tf_op jit(solution)/shard_map/ppermute | solution.py:10
  57.7 16.4 %collective-permute-start.14 = (bf16[2,64,768]{2,1,0:T(8,128)(2,1)S(1)}, bf16[2,64,768]{2,1,0:T(8,128)(2,1)S(1)}, u32[]{:S(2)}, u32[]{:S(2)}) collective-permute-start(bf16[2,64,768]{2,1,0:T(8,128)(2,1)S(1)} %pad_maximum_fusion.10), channel_id=1, source_target_pairs={{0,8},{1,9},{2,10},{3,11},{4,12},{5,13},{6,14},{7,15},{8,0},{9,1},... | collective-permute-start | bytes 589832 | tf_op jit(solution)/shard_map/ppermute | solution.py:10
  60.4 15.6 %collective-permute-start.1 = (bf16[2,128,768]{2,1,0:T(8,128)(2,1)S(1)}, bf16[2,128,768]{2,1,0:T(8,128)(2,1)S(1)}, u32[]{:S(2)}, u32[]{:S(2)}) collective-permute-start(bf16[2,128,768]{2,1,0:T(8,128)(2,1)S(1)} %pad_maximum_fusion.4), channel_id=1, source_target_pairs={{0,2},{1,3},{2,0},{3,1},{4,6},{5,7},{6,4},{7,5},{8,10},{9,11},{10,... | collective-permute-start | bytes 1179656 | tf_op jit(solution)/shard_map/ppermute | solution.py:10
  61.9 37.4 %collective-permute-start.5 = (bf16[2,128,768]{2,1,0:T(8,128)(2,1)}, bf16[2,128,768]{2,1,0:T(8,128)(2,1)}, u32[]{:S(2)}, u32[]{:S(2)}) collective-permute-start(bf16[2,128,768]{2,1,0:T(8,128)(2,1)} %pad_maximum_fusion.5), channel_id=1, source_target_pairs={{0,8},{1,9},{2,10},{3,11},{4,12},{5,13},{6,14},{7,15},{8,0},{9,1},... | collective-permute-start | bytes 1179656 | tf_op jit(solution)/shard_map/ppermute | solution.py:10
  63.1 11.0 %copy-start.5 = (bf16[2,64,768]{2,1,0:T(8,128)(2,1)}, bf16[2,64,768]{2,1,0:T(8,128)(2,1)S(1)}, u32[]{:S(2)}) copy-start(bf16[2,64,768]{2,1,0:T(8,128)(2,1)S(1)} %get-tuple-element.55) | copy-start | bytes 589828
  63.9 54.7 %collective-permute-start.10 = (bf16[2,128,768]{2,1,0:T(8,128)(2,1)}, bf16[2,128,768]{2,1,0:T(8,128)(2,1)}, u32[]{:S(2)}, u32[]{:S(2)}) collective-permute-start(bf16[2,128,768]{2,1,0:T(8,128)(2,1)} %pad_maximum_fusion.6), channel_id=1, source_target_pairs={{0,16},{1,17},{2,18},{3,19},{4,20},{5,21},{6,22},{7,23},{8,24},{9,... | collective-permute-start | bytes 1179656 | tf_op jit(solution)/shard_map/ppermute | solution.py:10
  74.9 47.8 %collective-permute-start.15 = (bf16[2,128,768]{2,1,0:T(8,128)(2,1)}, bf16[2,128,768]{2,1,0:T(8,128)(2,1)}, u32[]{:S(2)}, u32[]{:S(2)}) collective-permute-start(bf16[2,128,768]{2,1,0:T(8,128)(2,1)} %pad_maximum_fusion.7), channel_id=1, source_target_pairs={{0,16},{1,17},{2,18},{3,19},{4,20},{5,21},{6,22},{7,23},{8,24},{9,... | collective-permute-start | bytes 1179656 | tf_op jit(solution)/shard_map/ppermute | solution.py:10
  128.2 16.4 %copy-start.8 = (bf16[1,256,768]{2,1,0:T(8,128)(2,1)S(1)}, bf16[1,256,768]{2,1,0:T(8,128)(2,1)}, u32[]{:S(2)}) copy-start(bf16[1,256,768]{2,1,0:T(8,128)(2,1)} %get-tuple-element.47) | copy-start | bytes 1179652
  145.5 5.5 %copy-start.22 = (f32[256,12]{0,1:T(8,128)S(1)}, f32[256,12]{0,1:T(8,128)}, u32[]{:S(2)}) copy-start(f32[256,12]{0,1:T(8,128)} %get-tuple-element.33) | copy-start | bytes 36868
  145.5 5.5 %copy-start.23 = (f32[256,12]{0,1:T(8,128)S(1)}, f32[256,12]{0,1:T(8,128)}, u32[]{:S(2)}) copy-start(f32[256,12]{0,1:T(8,128)} %select_n.467) | copy-start | bytes 36868
  145.5 5.5 %copy-start.11 = (pred[256,256]{0,1:T(8,128)(4,1)S(1)}, pred[256,256]{0,1:T(8,128)(4,1)}, u32[]{:S(2)}) copy-start(pred[256,256]{0,1:T(8,128)(4,1)} %iota_compare_fusion) | copy-start | bytes 196612
  (24 other events, 68.1 us)
where the time goes:
time: 159 us; the launch traced here: 157 us
  local copies, waits for them, and re-layouts  71.2 us (45%)
  other arithmetic  39.9 us (25%)
  starting transfers between devices  19.3 us (12%)
  matrix products  17 us (11%)
  waiting for transfers between devices  8.93 us (6%)
    ppermute x16, starting transfers between devices, swapped(): return lax.ppermute(value, axis, pairs)  19.3 us
    mul x8, local copies, waits for them, and re-layouts, merge_levels(): level_out[:, None] * take_new[..., None]  17.3 us
    reshape x9, local copies, waits for them, and re-layouts, select_rows(): shaped = source.reshape(count // group, group, heads, head_size)  10.6 us
    dot_general x5, matrix products, attend_rows(): jnp.einsum('hqk,khd->qhd', weights.astype(jnp.bfloat16), value_heads, pre...  10.3 us
    reduce_sum x3, other arithmetic, select_rows(): jnp.sum(jnp.where(hit[None, :, :, None], shaped, jnp.zeros((), source.dty...  10.2 us
    unnamed x71, local copies, waits for them, and re-layouts  9.24 us
    ppermute x16, waiting for transfers between devices, swapped(): return lax.ppermute(value, axis, pairs)  8.93 us
    slice x4, local copies, waits for them, and re-layouts, body(): stacks[height][0]  6.92 us
  transfers between devices with their start and end apart: 16, of which 3 were waited for; matrix products, arithmetic and copies ran while one was open for 52% of the time, Pallas kernels for 0%

commit v1 on v0

v1 whole, which is shorter than its diff:
```python
import functools

import jax
import jax.numpy as jnp
from jax import lax
from jax.experimental import pallas as pl
from jax.experimental.pallas import tpu as pltpu
from jax.sharding import PartitionSpec as P

MESH = pl.DeviceIdType.MESH


def plan_of(levels, count, tokens, heads):
    plan = []
    shift = 0
    for height in range(1, levels):
        group = min(4**height, count)
        per = -(-heads // group)
        plan.append((height, group, tokens // group, per, shift % group))
        if per == 1:
            shift += heads
    return plan


def halves(shape):
    return lax.broadcasted_iota(jnp.int32, shape, 1) < shape[1] // 2


def swap_halves(value):
    return pltpu.roll(value.astype(jnp.float32), value.shape[1] // 2, 1)


def causal_unit(query, key, value):
    tokens = query.shape[0]
    half = tokens // 2
    outs, peaks = [], []
    for start in (0, half):
        end = start + half
        scores = lax.dot_general(
            query[start:end],
            key[:end],
            (((1,), (1,)), ((), ())),
            preferred_element_type=jnp.float32,
        )
        rows = lax.broadcasted_iota(jnp.int32, scores.shape, 0) + start
        cols = lax.broadcasted_iota(jnp.int32, scores.shape, 1)
        scores = jnp.where(cols <= rows, scores, -1e30)
        peak = jnp.max(scores, axis=1, keepdims=True)
        weights = jnp.exp(scores - peak).astype(jnp.bfloat16)
        outs.append(jnp.dot(weights, value[:end], preferred_element_type=jnp.float32))
        peaks.append(peak)
    return jnp.concatenate(outs, 0), jnp.concatenate(peaks, 0)


def exchange_kernel(plan, heads, scale, offs, q_ref, k_ref, v_ref, out_ref, *scratch):
    number = len(plan)
    stage = scratch[:number]
    inbox = scratch[number : 2 * number]
    outbox = scratch[2 * number : 3 * number]
    back = scratch[3 * number : 4 * number]
    numer, total, peaks, send_sem, recv_sem, ret_send, ret_recv = scratch[4 * number :]
    tokens = q_ref.shape[0]
    pair = 2 * (q_ref.shape[1] // heads)
    pairs = heads // 2
    me = lax.axis_index("ctx")
    count = lax.axis_size("ctx")

    barrier = pltpu.get_barrier_semaphore()

    def greet(step, carry):
        other = lax.rem(me + step, count)
        pl.semaphore_signal(barrier, inc=1, device_id=(other,), device_id_type=MESH)
        return carry

    lax.fori_loop(1, count, greet, 0)

    picked = sum(rows for _, _, rows, _, _ in plan)
    row_id = lax.broadcasted_iota(jnp.int32, (picked, tokens), 0)
    col_id = lax.broadcasted_iota(jnp.int32, (picked, tokens), 1)
    low_p = halves((picked, pair))

    def pick(p, carry):
        cols = pl.ds(pl.multiple_of(p * pair, pair), pair)
        packed = jnp.concatenate([q_ref[:, cols], k_ref[:, cols], v_ref[:, cols]], 1)
        for side in range(2):
            head = 2 * p + side
            first = 0
            target = jnp.zeros((picked, tokens), jnp.int32)
            for height, group, rows, _, _ in plan:
                here = (row_id - first) * group + offs[height, head]
                target = here if first == 0 else jnp.where(row_id < first, target, here)
                first += rows
            hit = jnp.where(col_id == target, 1.0, 0.0).astype(jnp.bfloat16)
            got = jnp.dot(hit, packed, preferred_element_type=jnp.float32)
            query, key, value = got[:, :pair], got[:, pair : 2 * pair], got[:, 2 * pair :]
            if side == 0:
                key = swap_halves(key)
            else:
                query, value = swap_halves(query), swap_halves(value)
            left = jnp.where(low_p, query * scale, key)
            right = jnp.where(low_p, value, 1.0)
            both = jnp.concatenate([left, right], 1)
            first = 0
            for at, (_, _, rows, _, _) in enumerate(plan):
                stage[at][head] = both[first : first + rows].astype(stage[at].dtype)
                first += rows
        return carry

    lax.fori_loop(0, pairs, pick, 0)
    pl.semaphore_wait(barrier, count - 1)

    def place(entry, head):
        _, group, _, per, shift = entry
        where = lax.rem(shift + head // per, group)
        mine = lax.rem(me, group)
        return me - mine + where, where == mine, mine, head % per

    def sending(at, head):
        owner, _, mine, slot = place(plan[at], head)
        return pltpu.make_async_remote_copy(
            src_ref=stage[at].at[head],
            dst_ref=inbox[at].at[slot, mine],
            send_sem=send_sem.at[at, head],
            recv_sem=recv_sem.at[at, slot],
            device_id=(owner,),
            device_id_type=MESH,
        )

    order = list(range(number))[::-1]
    for at in order:

        def push(head, carry, at=at):
            _, own, mine, slot = place(plan[at], head)

            @pl.when(jnp.logical_not(own))
            def _():
                sending(at, head).start()

            @pl.when(own)
            def _():
                inbox[at][slot, mine] = stage[at][head]

            return carry

        lax.fori_loop(0, heads, push, 0)

    low = halves((tokens, pair))

    def base(p, carry):
        cols = pl.ds(pl.multiple_of(p * pair, pair), pair)
        query = q_ref[:, cols].astype(jnp.float32) * scale
        key = k_ref[:, cols]
        value = v_ref[:, cols].astype(jnp.float32)
        got = []
        for side in range(2):
            mask = low if side == 0 else jnp.logical_not(low)
            got.append(
                causal_unit(
                    jnp.where(mask, query, 0.0).astype(jnp.bfloat16),
                    key,
                    jnp.where(mask, value, 1.0).astype(jnp.bfloat16),
                )
            )
        numer[:, cols] = jnp.where(low, got[0][0], got[1][0])
        total[:, cols] = swap_halves(jnp.where(low, got[1][0], got[0][0]))
        peaks[:, cols] = jnp.where(low, got[0][1], got[1][1])
        return carry

    lax.fori_loop(0, pairs, base, 0)

    lane = lax.broadcasted_iota(jnp.int32, (tokens, pair), 1)
    mid_lane = pair // 2

    def returning(at, slot, head, there):
        _, group, _, _, _ = plan[at]
        mine = lax.rem(me, group)
        return pltpu.make_async_remote_copy(
            src_ref=outbox[at].at[slot, there],
            dst_ref=back[at].at[head],
            send_sem=ret_send.at[at, slot],
            recv_sem=ret_recv.at[at, head],
            device_id=(me - mine + there,),
            device_id_type=MESH,
        )

    def owned(at, slot):
        _, group, _, per, shift = plan[at]
        mine = lax.rem(me, group)
        head = lax.rem(mine + group - shift, group) * per + slot
        return head, mine

    for at in order:
        _, group, rows, per, _ = plan[at]
        for slot in range(per):
            head, mine = owned(at, slot)

            @pl.when(head < heads)
            def _(at=at, group=group, rows=rows, slot=slot, head=head, mine=mine):
                arrived = inbox[at].at[slot, pl.ds(0, group - 1)]
                pltpu.make_async_copy(arrived, arrived, recv_sem.at[at, slot]).wait()
                block = inbox[at][slot].reshape(tokens, 2 * pair)
                left = block[:, :pair].astype(jnp.float32)
                query = jnp.where(low, left, 0.0).astype(jnp.bfloat16)
                key = swap_halves(left).astype(jnp.bfloat16)
                got, peak = causal_unit(query, key, block[:, pair:].astype(jnp.bfloat16))
                lse = peak + jnp.log(jnp.where(low, 1.0, got))
                hi = lse.astype(jnp.bfloat16).astype(jnp.float32)
                rest = lse - hi
                mid = rest.astype(jnp.bfloat16).astype(jnp.float32)
                parts = jnp.where(lane == mid_lane, hi, 0.0)
                parts = jnp.where(lane == mid_lane + 1, mid, parts)
                parts = jnp.where(lane == mid_lane + 2, rest - mid, parts)
                result = jnp.where(low, got / jnp.where(low, swap_halves(got), 1.0), parts)
                outbox[at][slot] = result.reshape(group, rows, pair).astype(outbox[at].dtype)

                def give(step, carry):
                    returning(at, slot, head, lax.rem(mine + step, group)).start()
                    return carry

                lax.fori_loop(1, group, give, 0)
                back[at][head] = outbox[at][slot, mine]

    def collect(at):
        def one(head, carry):
            _, own, mine, slot = place(plan[at], head)

            @pl.when(jnp.logical_not(own))
            def _():
                sending(at, head).wait_send()
                returning(at, slot, head, mine).wait_recv()

            return carry

        lax.fori_loop(0, heads, one, 0)

    for at in order:
        collect(at)

    token = lax.broadcasted_iota(jnp.int32, (tokens, 1), 0)

    def merge(p, carry):
        cols = pl.ds(pl.multiple_of(p * pair, pair), pair)
        values, lses = [], []
        for at, (height, group, rows, _, _) in enumerate(plan):
            spread = lax.broadcasted_iota(jnp.int32, (tokens, rows), 0)
            source = lax.broadcasted_iota(jnp.int32, (tokens, rows), 1)
            got, lse = [], []
            for side in range(2):
                head = 2 * p + side
                offset = offs[height, head]
                hit = jnp.where(spread == source * group + offset, 1.0, 0.0).astype(jnp.bfloat16)
                sent = back[at][head]
                if side == 1:
                    sent = swap_halves(sent)
                moved = jnp.dot(hit, sent.astype(jnp.bfloat16), preferred_element_type=jnp.float32)
                other = jnp.logical_not(low) if side == 0 else low
                level_lse = jnp.sum(jnp.where(other, moved, 0.0), axis=1, keepdims=True)
                kept = lax.rem(token, group) == offset
                lse.append(jnp.where(kept, level_lse, -1e30))
                got.append(moved)
            values.append(jnp.where(low, got[0], got[1]))
            lses.append(jnp.where(low, lse[0], lse[1]))
        best = peaks[:, cols]
        for lse in lses:
            best = jnp.maximum(best, lse)
        keep = jnp.exp(peaks[:, cols] - best)
        top = numer[:, cols] * keep
        bottom = total[:, cols] * keep
        for value, lse in zip(values, lses):
            share = jnp.exp(lse - best)
            top = top + value * share
            bottom = bottom + share
        out_ref[:, cols] = (top / bottom).astype(out_ref.dtype)
        return carry

    lax.fori_loop(0, pairs, merge, 0)

    for at in order:
        _, group, _, per, _ = plan[at]
        for slot in range(per):
            head, _ = owned(at, slot)

            @pl.when(head < heads)
            def _(at=at, group=group, slot=slot):
                gone = outbox[at].at[slot, pl.ds(0, group - 1)]
                pltpu.make_async_copy(gone, gone, ret_send.at[at, slot]).wait()


def exchange_body(queries, keys, values, offsets):
    tokens, model = queries.shape
    levels, heads = offsets.shape
    count = lax.axis_size("ctx")
    plan = plan_of(levels, count, tokens, heads)
    pair = 2 * (model // heads)
    number = len(plan)
    most = max(entry[3] for entry in plan)

    def dtype(rows):
        return jnp.bfloat16 if rows % 8 == 0 else jnp.float32

    scratch = []
    for _, group, rows, per, _ in plan:
        scratch.append(pltpu.VMEM((heads, rows, 2 * pair), dtype(rows)))
    for _, group, rows, per, _ in plan:
        scratch.append(pltpu.VMEM((per, group, rows, 2 * pair), dtype(rows)))
    for _, group, rows, per, _ in plan:
        scratch.append(pltpu.VMEM((per, group, rows, pair), dtype(rows)))
    for _, group, rows, per, _ in plan:
        scratch.append(pltpu.VMEM((heads, rows, pair), dtype(rows)))
    scratch += [pltpu.VMEM((tokens, model), jnp.float32)] * 3
    scratch += [
        pltpu.SemaphoreType.DMA((number, heads)),
        pltpu.SemaphoreType.DMA((number, most)),
        pltpu.SemaphoreType.DMA((number, most)),
        pltpu.SemaphoreType.DMA((number, heads)),
    ]
    scale = (model // heads) ** -0.5
    vmem = pl.BlockSpec(memory_space=pltpu.VMEM)
    return pl.pallas_call(
        functools.partial(exchange_kernel, plan, heads, scale),
        out_shape=jax.ShapeDtypeStruct((tokens, model), jnp.bfloat16),
        in_specs=[pl.BlockSpec(memory_space=pltpu.SMEM), vmem, vmem, vmem],
        out_specs=vmem,
        scratch_shapes=scratch,
        compiler_params=pltpu.CompilerParams(collective_id=0, has_side_effects=True),
    )(offsets, queries, keys, values)


def solution(mesh):
    in_specs = (P("ctx", None), P("ctx", None), P("ctx", None), P())
    out_specs = P("ctx", None)
    return jax.shard_map(
        exchange_body, mesh=mesh, in_specs=in_specs, out_specs=out_specs, check_vma=False
    )
```

time: 159 us -> 29.2 us (0.18); the launches traced: 157 us -> 29.1 us
  local copies, waits for them, and re-layouts: 71.2 us -> 1.77 us
  other arithmetic: 39.9 us -> 0 us
  Pallas kernels: 0 us -> 27.3 us
  starting transfers between devices: 19.3 us -> 0 us
  matrix products: 17 us -> 0 us
  waiting for transfers between devices: 8.93 us -> 0 us
    pallas_call x0 -> x1, Pallas kernels: none -> 27.3 us  [exchange_body(): pl.pallas_call(functools.partial(exchange_kernel, plan, heads, scale), ou...]
    ppermute x16 -> x0, starting transfers between devices: 19.3 us -> none  [swapped(): return lax.ppermute(value, axis, pairs)]
    mul x8 -> x0, local copies, waits for them, and re-layouts: 17.3 us -> none  [merge_levels(): level_out[:, None] * take_new[..., None]]
    dot_general x10 -> x0, matrix products: 17 us -> none  [the longest x5 10.3 us: attend_rows(): jnp.einsum('hqk,khd->qhd', weights.astype(jnp.bfloat16), value_heads, pre...]
    reduce_sum x7 -> x0, other arithmetic: 15 us -> none  [the longest x3 10.2 us: select_rows(): jnp.sum(jnp.where(hit[None, :, :, None], shaped, jnp.zeros((), source.dty...]
    slice x9 -> x0, local copies, waits for them, and re-layouts: 14.5 us -> none  [the longest x4 6.92 us: body(): stacks[height][0]]
    select_n x20 -> x0, other arithmetic: 13.1 us -> none  [the longest x15 6.3 us: place_pair(): first = jnp.where(upper, arrived, mine)]
    reshape x9 -> x0, local copies, waits for them, and re-layouts: 10.6 us -> none  [select_rows(): shaped = source.reshape(count // group, group, heads, head_size)]
  transfers between devices with their start and end apart: 16 -> 0, of which waited for: 3 -> 0; matrix products, arithmetic and copies ran while one was open for 52% -> 0% of each run, Pallas kernels for 0% -> 0%
where the time goes in v1:
time: 29.2 us; the launch traced here: 29.1 us
  Pallas kernels  27.3 us (93%)
  local copies, waits for them, and re-layouts  1.77 us (6%)
    pallas_call x1, Pallas kernels, exchange_body(): pl.pallas_call(functools.partial(exchange_kernel, plan, heads, scale), ou...  27.3 us
    unnamed x1, local copies, waits for them, and re-layouts  1.77 us

profile of v1, /device:TPU:0, one launch (start us, length us, event | category | flops | bytes accessed | tf_op | source)
XLA Modules:
  0.0 29.1 jit_solution(17497740451510191566)
XLA Ops:
  0.0 27.3 %shard_map.46 = bf16[256,768]{1,0:T(8,128)(2,1)} custom-call(s32[5,12]{1,0:T(8,128)} %offs.1, bf16[256,768]{1,0:T(8,128)(2,1)} %q_ref.1, bf16[256,768]{1,0:T(8,128)(2,1)} %k_ref.1, bf16[256,768]{1,0:T(8,128)(2,1)} %v_ref.1), custom_call_target="tpu_custom_call" | custom-call | tf_op jit(solution)/shard_map/pallas_call | solution.py:319
  27.3 1.8 %copy.6 = bf16[256,768]{1,0:T(8,128)(2,1)} copy(bf16[256,768]{1,0:T(8,128)(2,1)} %shard_map.46) | data formatting | bytes 786432

commit v2 on v1

--- a/solution.py
+++ b/solution.py
@@ -12,14 +12,20 @@
 
 def plan_of(levels, count, tokens, heads):
     plan = []
-    shift = 0
+    late = False
     for height in range(1, levels):
         group = min(4**height, count)
         per = -(-heads // group)
-        plan.append((height, group, tokens // group, per, shift % group))
-        if per == 1:
-            shift += heads
+        shift = 0
+        if group >= 2 * heads:
+            shift = group // 4 + (group // 2 - heads if late else 0)
+            late = not late
+        plan.append((height, group, tokens // group, per, shift))
     return plan
+
+
+def is_packed(rows):
+    return rows % 32 == 0
 
 
 def halves(shape):
@@ -67,12 +73,27 @@
 
     barrier = pltpu.get_barrier_semaphore()
 
+    def owns(device, entry):
+        _, group, _, per, shift = entry
+        return lax.rem(lax.rem(device, group) + group - shift, group) * per < heads
+
     def greet(step, carry):
         other = lax.rem(me + step, count)
-        pl.semaphore_signal(barrier, inc=1, device_id=(other,), device_id_type=MESH)
-        return carry
-
-    lax.fori_loop(1, count, greet, 0)
+        meets = False
+        for entry in plan:
+            group = entry[1]
+            same = lax.div(me, group) == lax.div(other, group)
+            meets = jnp.logical_or(
+                meets, jnp.logical_and(same, jnp.logical_or(owns(me, entry), owns(other, entry)))
+            )
+
+        @pl.when(meets)
+        def _():
+            pl.semaphore_signal(barrier, inc=1, device_id=(other,), device_id_type=MESH)
+
+        return carry + jnp.where(meets, 1, 0)
+
+    partners = lax.fori_loop(1, count, greet, 0)
 
     picked = sum(rows for _, _, rows, _, _ in plan)
     row_id = lax.broadcasted_iota(jnp.int32, (picked, tokens), 0)
@@ -93,21 +114,32 @@
             hit = jnp.where(col_id == target, 1.0, 0.0).astype(jnp.bfloat16)
             got = jnp.dot(hit, packed, preferred_element_type=jnp.float32)
             query, key, value = got[:, :pair], got[:, pair : 2 * pair], got[:, 2 * pair :]
+            swapped = swap_halves(value)
             if side == 0:
                 key = swap_halves(key)
             else:
-                query, value = swap_halves(query), swap_halves(value)
+                query = swap_halves(query)
+                value, swapped = swapped, value
             left = jnp.where(low_p, query * scale, key)
-            right = jnp.where(low_p, value, 1.0)
-            both = jnp.concatenate([left, right], 1)
             first = 0
             for at, (_, _, rows, _, _) in enumerate(plan):
-                stage[at][head] = both[first : first + rows].astype(stage[at].dtype)
-                first += rows
+                kind = stage[at].dtype
+                last = first + rows
+                if is_packed(rows):
+                    middle = first + rows // 2
+                    right = jnp.where(
+                        low_p[: rows // 2], value[first:middle], swapped[middle:last]
+                    )
+                    stage[at][head] = jnp.concatenate([left[first:last], right], 0).astype(kind)
+                else:
+                    stage[at][head] = jnp.concatenate(
+                        [left[first:last], value[first:last]], 1
+                    ).astype(kind)
+                first = last
         return carry
 
     lax.fori_loop(0, pairs, pick, 0)
-    pl.semaphore_wait(barrier, count - 1)
+    pl.semaphore_wait(barrier, partners)
 
     def place(entry, head):
         _, group, _, per, shift = entry
@@ -166,7 +198,7 @@
         peaks[:, cols] = jnp.where(low, got[0][1], got[1][1])
         return carry
 
-    lax.fori_loop(0, pairs, base, 0)
+    lax.fori_loop(0, 2 * pairs // 3, base, 0)
 
     lane = lax.broadcasted_iota(jnp.int32, (tokens, pair), 1)
     mid_lane = pair // 2
@@ -198,11 +230,22 @@
             def _(at=at, group=group, rows=rows, slot=slot, head=head, mine=mine):
                 arrived = inbox[at].at[slot, pl.ds(0, group - 1)]
                 pltpu.make_async_copy(arrived, arrived, recv_sem.at[at, slot]).wait()
-                block = inbox[at][slot].reshape(tokens, 2 * pair)
-                left = block[:, :pair].astype(jnp.float32)
+                block = inbox[at][slot]
+                if is_packed(rows):
+                    left = block[:, :rows].reshape(tokens, pair).astype(jnp.float32)
+                    right = block[:, rows:].reshape(tokens // 2, pair).astype(jnp.float32)
+                    split = (group, rows // 2, pair)
+                    right = jnp.concatenate(
+                        [right.reshape(split), swap_halves(right).reshape(split)], 1
+                    ).reshape(tokens, pair)
+                else:
+                    block = block.reshape(tokens, 2 * pair)
+                    left = block[:, :pair].astype(jnp.float32)
+                    right = block[:, pair:].astype(jnp.float32)
+                value = jnp.where(low, right, 1.0).astype(jnp.bfloat16)
                 query = jnp.where(low, left, 0.0).astype(jnp.bfloat16)
                 key = swap_halves(left).astype(jnp.bfloat16)
-                got, peak = causal_unit(query, key, block[:, pair:].astype(jnp.bfloat16))
+                got, peak = causal_unit(query, key, value)
                 lse = peak + jnp.log(jnp.where(low, 1.0, got))
                 hi = lse.astype(jnp.bfloat16).astype(jnp.float32)
                 rest = lse - hi
@@ -219,6 +262,8 @@
 
                 lax.fori_loop(1, group, give, 0)
                 back[at][head] = outbox[at][slot, mine]
+
+    lax.fori_loop(2 * pairs // 3, pairs, base, 0)
 
     def collect(at):
         def one(head, carry):
@@ -255,7 +300,7 @@
                 moved = jnp.dot(hit, sent.astype(jnp.bfloat16), preferred_element_type=jnp.float32)
                 other = jnp.logical_not(low) if side == 0 else low
                 level_lse = jnp.sum(jnp.where(other, moved, 0.0), axis=1, keepdims=True)
-                kept = lax.rem(token, group) == offset
+                kept = jnp.bitwise_and(token, group - 1) == offset
                 lse.append(jnp.where(kept, level_lse, -1e30))
                 got.append(moved)
             values.append(jnp.where(low, got[0], got[1]))
@@ -273,7 +318,7 @@
         out_ref[:, cols] = (top / bottom).astype(out_ref.dtype)
         return carry
 
-    lax.fori_loop(0, pairs, merge, 0)
+    lax.fori_loop(0, pairs, merge, 0, unroll=2)
 
     for at in order:
         _, group, _, per, _ = plan[at]
@@ -298,11 +343,14 @@
     def dtype(rows):
         return jnp.bfloat16 if rows % 8 == 0 else jnp.float32
 
+    def block(rows):
+        return (rows + rows // 2, pair) if is_packed(rows) else (rows, 2 * pair)
+
     scratch = []
     for _, group, rows, per, _ in plan:
-        scratch.append(pltpu.VMEM((heads, rows, 2 * pair), dtype(rows)))
+        scratch.append(pltpu.VMEM((heads, *block(rows)), dtype(rows)))
     for _, group, rows, per, _ in plan:
-        scratch.append(pltpu.VMEM((per, group, rows, 2 * pair), dtype(rows)))
+        scratch.append(pltpu.VMEM((per, group, *block(rows)), dtype(rows)))
     for _, group, rows, per, _ in plan:
         scratch.append(pltpu.VMEM((per, group, rows, pair), dtype(rows)))
     for _, group, rows, per, _ in plan:

time: 29.2 us -> 27.2 us (0.932)
  the two profiles are of different devices: /device:TPU:0 before, /device:TPU:17 now
where the time goes in v2:
time: 27.2 us; the launch traced here: 27.1 us
  Pallas kernels  25.3 us (93%)
  local copies, waits for them, and re-layouts  1.77 us (7%)
    pallas_call x1, Pallas kernels, exchange_body(): pl.pallas_call(functools.partial(exchange_kernel, plan, heads, scale), ou...  25.3 us
    unnamed x1, local copies, waits for them, and re-layouts  1.77 us

profile of v2, /device:TPU:17, one launch (start us, length us, event | category | flops | bytes accessed | tf_op | source)
XLA Modules:
  0.0 27.1 jit_solution(8210419379161999999)
XLA Ops:
  0.0 25.3 %shard_map.46 = bf16[256,768]{1,0:T(8,128)(2,1)} custom-call(s32[5,12]{1,0:T(8,128)} %offs.1, bf16[256,768]{1,0:T(8,128)(2,1)} %q_ref.1, bf16[256,768]{1,0:T(8,128)(2,1)} %k_ref.1, bf16[256,768]{1,0:T(8,128)(2,1)} %v_ref.1), custom_call_target="tpu_custom_call" | custom-call | tf_op jit(solution)/shard_map/pallas_call | solution.py:367
  25.3 1.8 %copy.6 = bf16[256,768]{1,0:T(8,128)(2,1)} copy(bf16[256,768]{1,0:T(8,128)(2,1)} %shard_map.46) | data formatting | bytes 786432
